TPU v7x, 32 devices: a whole 2x2x4 slice. The times are simulated.
32 devices in a mesh: chip: 2 (over y), board: 4 (over z), cuts: 4 (over x, core).
Axes of the slice: x: 2, y: 2, z: 4, core: 2. Of those that a mesh axis runs over, the one named last changes fastest.
Arguments:
- features: bfloat16 [32, 2048, 1024], P(('chip', 'board', 'cuts')), may hold values from -6 to 6
- targets: bfloat16 [32, 2048, 256], P(('chip', 'board', 'cuts')), may hold values from -24 to 24
- lower_weight: bfloat16 [32, 1024, 512], P(('chip', 'board', 'cuts')), may hold values from -0.1875 to 0.1875
- head_weight: float32 [32, 512, 256], P(('chip', 'board', 'cuts')), may hold values from -0.25 to 0.25
- batch_rows: int32 [32, 2, 1024], P(('chip', 'board', 'cuts')), may hold values from 0 to 2047
- sample_counts: int32 [32], P(('chip', 'board', 'cuts')), may hold values from 1 to 1000
- cluster_ids: int32 [32], P(('chip', 'board', 'cuts')), may hold values from 0 to 7, as said below
Outputs:
- cluster_step: float32 [32, 512, 256], P(('chip', 'board', 'cuts'))
Inputs may be any that keep to these rules, and one draw needn't show every extreme that they name: `cluster_ids`: every one of the 8 clusters has at least one client.
All inputs are finite; a program needn't handle non-finite values.
Results may differ from a plain program's by a relative error of at most 0.0003.
Values sent between devices are 32-bit elements; how exact they have to be, the bound alone decides.
A program may use at most 64 MiB of HBM per device.

v0:
```python
import jax
import jax.numpy as jnp
from jax import lax
from jax.sharding import PartitionSpec as P

LR = 0.5


def on_device(features, targets, lower_weight, head_weight, batch_rows, sample_counts, cluster_ids):
    hidden = jnp.tanh(jnp.dot(features[0], lower_weight[0], preferred_element_type=jnp.float32))
    start = head_weight[0]
    weight = start
    count_rows = batch_rows.shape[2]
    for step in range(batch_rows.shape[1]):
        picked = jnp.take(hidden, batch_rows[0, step], axis=0)
        wanted = jnp.take(targets[0], batch_rows[0, step], axis=0).astype(jnp.float32)
        err = jnp.dot(picked, weight, precision=lax.Precision.HIGHEST) - wanted
        grad = jnp.dot(picked.T, err, precision=lax.Precision.HIGHEST) / count_rows
        weight = weight - LR * grad
    delta = weight - start
    cluster = cluster_ids[0]
    number = 8
    chip_count = lax.axis_size("chip")
    rest_count = lax.axis_size(("board", "cuts"))
    every_id, every_count = (
        lax.all_gather(cluster_ids, ("chip", "board", "cuts"), axis=0, tiled=True),
        lax.all_gather(sample_counts, ("chip", "board", "cuts"), axis=0, tiled=True),
    )
    table = (every_id[:, None] == jnp.arange(number, dtype=jnp.int32)[None, :]).astype(jnp.float32)
    weighted = table * every_count.astype(jnp.float32)[:, None]
    counts = jnp.sum(weighted, axis=0)
    scaled = (sample_counts[0].astype(jnp.float32) * delta).reshape(chip_count, rest_count, -1)
    columns = lax.all_to_all(
        lax.all_to_all(scaled, "chip", split_axis=0, concat_axis=0, tiled=True),
        ("board", "cuts"),
        split_axis=1,
        concat_axis=1,
        tiled=True,
    )
    columns = columns.reshape(chip_count * rest_count, -1)
    share = jnp.dot(table.T, columns, precision=lax.Precision.HIGHEST)
    outgoing = jnp.dot(table, share, precision=lax.Precision.HIGHEST)
    outgoing = outgoing.reshape(chip_count, rest_count, -1)
    arrived = lax.all_to_all(
        lax.all_to_all(outgoing, "chip", split_axis=0, concat_axis=0, tiled=True),
        ("board", "cuts"),
        split_axis=1,
        concat_axis=1,
        tiled=True,
    )
    mine = arrived.reshape(delta.shape)
    denom = lax.dynamic_index_in_dim(counts, cluster, 0, keepdims=False)
    return (mine / (LR * denom))[None]


def solution(mesh):
    return jax.shard_map(
        on_device,
        mesh=mesh,
        in_specs=(
            P(("chip", "board", "cuts"), None, None),
            P(("chip", "board", "cuts"), None, None),
            P(("chip", "board", "cuts"), None, None),
            P(("chip", "board", "cuts"), None, None),
            P(("chip", "board", "cuts"), None, None),
            P(("chip", "board", "cuts")),
            P(("chip", "board", "cuts")),
        ),
        out_specs=P(("chip", "board", "cuts"), None, None),
        check_vma=False,
    )
```

profile of v0, /device:TPU:0, one launch (start us, length us, event | category | flops | bytes accessed | tf_op | source)
XLA Modules:
  0.0 138.6 jit_solution(8541357281149164295)
XLA Ops:
  0.0 0.0 copy-start
  0.0 0.8 fusion.57
  0.8 0.4 copy-done
  1.3 6.5 %fusion.2 = f32[2048,512]{1,0:T(8,128)} fusion(bf16[1,2048,1024]{2,1,0:T(8,128)(2,1)} %param.11, bf16[1,1024,512]{2,1,0:T(8,128)(2,1)S(1)} %copy-done), kind=kOutput, calls=%fused_computation.6 | convolution fusion | flops 2147483648 | bytes 9437184 | tf_op jit(solution)/shard_map/dot_general | solution.py:10
  7.7 0.0 copy-start.1
  7.7 7.5 %gather_fusion = f32[1024,512]{1,0:T(8,128)} fusion(f32[2048,512]{1,0:T(8,128)} %fusion.2, s32[1024]{0:T(1024)S(1)} %fusion.49), kind=kCustom, calls=%fused_computation.clone | custom fusion | bytes 4198400 | tf_op jit(solution)/shard_map/jit(_take)/gather | solution.py:15
  15.3 0.0 copy-done.1
  15.3 5.0 %gather_fusion.1 = bf16[1024,256]{1,0:T(8,128)(2,1)} fusion(bf16[2048,256]{1,0:T(8,128)(2,1)S(1)} %bitcast.29, s32[1024]{0:T(1024)S(1)} %fusion.49), kind=kCustom, calls=%fused_computation.1.clone | custom fusion | bytes 1052672 | tf_op jit(solution)/shard_map/jit(_take)/gather | solution.py:16
  20.2 7.5 %gather_fusion.2 = f32[1024,512]{1,0:T(8,128)} fusion(f32[2048,512]{1,0:T(8,128)} %fusion.2, s32[1024]{0:T(1024)S(1)} %fusion.50), kind=kCustom, calls=%fused_computation.2.clone | custom fusion | bytes 4198400 | tf_op jit(solution)/shard_map/jit(_take)/gather | solution.py:15
  27.7 0.0 copy-start.4
  27.7 3.9 %gather_fusion.3 = bf16[1024,256]{1,0:T(8,128)(2,1)S(1)} fusion(bf16[2048,256]{1,0:T(8,128)(2,1)S(1)} %bitcast.30, s32[1024]{0:T(1024)S(1)} %fusion.50), kind=kCustom, calls=%fused_computation.3.clone | custom fusion | bytes 1052672 | tf_op jit(solution)/shard_map/jit(_take)/gather | solution.py:16
  31.7 0.0 copy-done.4
  31.7 0.0 copy-start.2
  31.7 3.7 %fusion.13 = f32[1024,256]{1,0:T(8,128)S(1)} fusion(f32[1024,512]{1,0:T(8,128)} %gather_fusion, pred[1024]{0:T(1024)(128)(4,1)S(1)} %compare_and_fusion.1, f32[1,512,256]{2,1,0:T(8,128)S(1)} %copy-done.4, bf16[1024,256]{1,0:T(8,128)(2,1)} %gather_fusion.1), kind=kOutput, calls=%fused_computation.15 | convolution fusion | flops 1611923456 | bytes 4195328 | tf_op jit(solution)/shard_map/dot_general | solution.py:17
  35.4 0.0 copy-done.2
  35.4 0.0 copy-start.3
  35.4 3.6 %fusion.34 = f32[512,256]{1,0:T(8,128)S(1)} fusion(f32[1024,256]{1,0:T(8,128)S(1)} %fusion.13, f32[1024,512]{1,0:T(8,128)S(1)} %copy-done.2, pred[1024]{0:T(1024)(128)(4,1)S(1)} %compare_and_fusion.1, f32[1,512,256]{2,1,0:T(8,128)S(1)} %copy-done.4), kind=kOutput, calls=%fused_computation.22 | convolution fusion | flops 1611399168 | bytes 4195328 | tf_op jit(solution)/shard_map/dot_general | solution.py:18
  39.7 0.0 copy-done.3
  39.7 2.4 %fusion.16 = f32[1024,256]{1,0:T(8,128)S(1)} fusion(f32[512,256]{1,0:T(8,128)S(1)} %fusion.34, f32[1024,512]{1,0:T(8,128)S(1)} %copy-done.3, pred[1024]{0:T(1024)(128)(4,1)S(1)} %compare_and_fusion, bf16[1024,256]{1,0:T(8,128)(2,1)S(1)} %gather_fusion.3), kind=kOutput, calls=%fused_computation.16 | convolution fusion | flops 1611923456 | bytes 4195328 | tf_op jit(solution)/shard_map/dot_general | solution.py:17
  42.1 3.6 %fusion.31 = f32[512,256]{1,0:T(8,128)S(1)} fusion(f32[512,256]{1,0:T(8,128)S(1)} %fusion.34, f32[1024,256]{1,0:T(8,128)S(1)} %fusion.16, f32[1024,512]{1,0:T(8,128)S(1)} %copy-done.3, pred[1024]{0:T(1024)(128)(4,1)S(1)} %compare_and_fusion, f32[1,512,256]{2,1,0:T(8,128)S(1)} %copy-done.4, f32[]{:T(128)} %bitcast), kind=kOutput, calls=%fused_computation.21 | convolution fusion | flops 1611661312 | bytes 4719620 | tf_op jit(solution)/shard_map/dot_general | solution.py:18
  45.8 0.1 reshape.37
  45.9 12.1 %all_to_all.20 = f32[2,16,4096]{2,1,0:T(8,128)S(1)} all-to-all(f32[2,16,4096]{2,1,0:T(8,128)S(1)} %reshape.37), channel_id=1, replica_groups=mesh['chip'=2,'board'=4,'cuts'=4] {'chip'}, dimensions={0} | all-to-all | bytes 1048576 | tf_op jit(solution)/shard_map/all_to_all | solution.py:34
  58.0 1.2 copy.22
  59.2 5.9 %all-to-all-start.1 = ((f32[2,16,4096]{2,0,1:T(2,128)}), f32[2,16,4096]{2,0,1:T(2,128)S(1)}, u32[]{:S(2)}, u32[]{:S(2)}) async-start(f32[2,16,4096]{2,0,1:T(2,128)} %copy.22), calls=%async_computation.1 | async-start | bytes 1048576 | tf_op jit(solution)/shard_map/all_to_all | solution.py:33
  65.8 0.1 dynamic-update-slice.1
  65.9 0.1 dynamic-update-slice
  66.0 40.0 %all-reduce.2 = (s32[32]{0:T(128)S(1)}, s32[32]{0:T(128)S(1)}) all-reduce(s32[32]{0:T(128)S(1)} %dynamic-update-slice, s32[32]{0:T(128)S(1)} %dynamic-update-slice.1), channel_id=1, replica_groups=mesh['chip'=2,'board'=4,'cuts'=4] {'chip','board','cuts'}, use_global_device_ids=true, to_apply=%add | all-reduce | flops 64 | bytes 512
  106.0 0.0 all-to-all-done.1
  106.0 0.3 copy.23
  106.3 0.3 fusion.48
  106.6 0.4 fusion.47
  107.0 10.5 %all_to_all.21 = f32[2,16,4096]{2,1,0:T(8,128)S(1)} all-to-all(f32[2,16,4096]{2,1,0:T(8,128)S(1)} %bitcast.32), channel_id=1, replica_groups=mesh['chip'=2,'board'=4,'cuts'=4] {'chip'}, dimensions={0} | all-to-all | bytes 1048576 | tf_op jit(solution)/shard_map/all_to_all | solution.py:45
  117.5 1.2 copy.24
  118.7 4.4 %all-to-all-start.3 = ((f32[2,16,4096]{2,0,1:T(2,128)}), f32[2,16,4096]{2,0,1:T(2,128)S(1)}, u32[]{:S(2)}, u32[]{:S(2)}) async-start(f32[2,16,4096]{2,0,1:T(2,128)} %copy.24), calls=%async_computation.3 | async-start | bytes 1048576 | tf_op jit(solution)/shard_map/all_to_all | solution.py:44
  123.2 0.1 select_reduce_fusion
  123.3 0.6 dynamic_slice.4
  124.4 13.0 %all-to-all-done.3 = f32[2,16,4096]{2,0,1:T(2,128)S(1)} async-done(((f32[2,16,4096]{2,0,1:T(2,128)}), f32[2,16,4096]{2,0,1:T(2,128)S(1)}, u32[]{:S(2)}, u32[]{:S(2)}) %all-to-all-start.3) | async-done | bytes 524320 | tf_op jit(solution)/shard_map/all_to_all | solution.py:44
  137.4 0.3 copy_divide_fusion
  137.7 0.9 div.20
  (7 shorter events, 0.0 us)
Async XLA Ops:
  0.0 1.3 copy-start
  7.7 7.5 %copy-start.1 = (bf16[1,2048,256]{2,1,0:T(8,128)(2,1)S(1)}, bf16[1,2048,256]{2,1,0:T(8,128)(2,1)}, u32[]{:S(2)}) copy-start(bf16[1,2048,256]{2,1,0:T(8,128)(2,1)} %param.12) | copy-start | bytes 3145732
  27.7 4.0 %copy-start.4 = (f32[1,512,256]{2,1,0:T(8,128)S(1)}, f32[1,512,256]{2,1,0:T(8,128)}, u32[]{:S(2)}) copy-start(f32[1,512,256]{2,1,0:T(8,128)} %param.14) | copy-start | bytes 1572868
  31.7 3.7 %copy-start.2 = (f32[1024,512]{1,0:T(8,128)S(1)}, f32[1024,512]{1,0:T(8,128)}, u32[]{:S(2)}) copy-start(f32[1024,512]{1,0:T(8,128)} %gather_fusion) | copy-start | bytes 6291460
  35.4 4.3 %copy-start.3 = (f32[1024,512]{1,0:T(8,128)S(1)}, f32[1024,512]{1,0:T(8,128)}, u32[]{:S(2)}) copy-start(f32[1024,512]{1,0:T(8,128)} %gather_fusion.2) | copy-start | bytes 6291460
  59.2 46.8 %all-to-all-start.1 = ((f32[2,16,4096]{2,0,1:T(2,128)}), f32[2,16,4096]{2,0,1:T(2,128)S(1)}, u32[]{:S(2)}, u32[]{:S(2)}) async-start(f32[2,16,4096]{2,0,1:T(2,128)} %copy.22), calls=%async_computation.1 | async-start | bytes 1048576 | tf_op jit(solution)/shard_map/all_to_all | solution.py:33
  118.7 18.7 %all-to-all-start.3 = ((f32[2,16,4096]{2,0,1:T(2,128)}), f32[2,16,4096]{2,0,1:T(2,128)S(1)}, u32[]{:S(2)}, u32[]{:S(2)}) async-start(f32[2,16,4096]{2,0,1:T(2,128)} %copy.24), calls=%async_computation.3 | async-start | bytes 1048576 | tf_op jit(solution)/shard_map/all_to_all | solution.py:44
where the time goes:
time: 139 us
  blocking collectives  62.6 us (45%)
  local copies, waits for them, and re-layouts  29.7 us (21%)
  matrix products  20.5 us (15%)
  waiting for transfers between devices  13 us (9%)
  starting transfers between devices  10.4 us (7%)
  between operations  2.04 us (1%)
    unnamed x1, blocking collectives  40 us
    gather x2, local copies, waits for them, and re-layouts, on_device(): picked = jnp.take(hidden, batch_rows[0, step], axis=0)  15 us
    all_to_all x1, waiting for transfers between devices, on_device(): lax.all_to_all(lax.all_to_all(outgoing, 'chip', split_axis=0, concat_axis...  13 us
    all_to_all x1, blocking collectives, on_device(): lax.all_to_all(scaled, 'chip', split_axis=0, concat_axis=0, tiled=True)  12.1 us
    all_to_all x1, blocking collectives, on_device(): lax.all_to_all(outgoing, 'chip', split_axis=0, concat_axis=0, tiled=True)  10.5 us
    gather x2, local copies, waits for them, and re-layouts, on_device(): jnp.take(targets[0], batch_rows[0, step], axis=0).astype(jnp.float32)  8.91 us
    dot_general x2, matrix products, on_device(): grad = jnp.dot(picked.T, err, precision=lax.Precision.HIGHEST) / count_rows  7.26 us
    dot_general x1, matrix products, on_device(): jnp.dot(features[0], lower_weight[0], preferred_element_type=jnp.float32)  6.46 us
  transfers between devices with their start and end apart: 2, of which 1 were waited for; matrix products, arithmetic and copies ran while one was open for 1% of the time, Pallas kernels for 0%

commit v1 on v0

v1 whole, which is shorter than its diff:
```python
import functools

import jax
import jax.numpy as jnp
from jax import lax
from jax.experimental import pallas as pl
from jax.experimental.pallas import tpu as pltpu
from jax.sharding import PartitionSpec as P

LR = 0.5
CLUSTERS = 8
LANES = 128
TILE = 256
CHUNKS = 8
LAG = 2
MESH = pl.DeviceIdType.MESH


def halves(value):
    high = value.astype(jnp.bfloat16)
    low = (value - high.astype(jnp.float32)).astype(jnp.bfloat16)
    return high, low


def dot(a, b):
    return jnp.dot(a, b, preferred_element_type=jnp.float32)


def dot_rows(a, b):
    return lax.dot_general(a, b, (((0,), (0,)), ((), ())), preferred_element_type=jnp.float32)


def local_kernel(x_hbm, lower_ref, target_ref, head_ref, rows_ref, delta_ref, x_buf, hid_hi, hid_lo, drawn, w_hi, w_lo, x_sem):
    pool = x_buf.shape[0]
    tile = min(TILE, pool)
    tiles = pool // tile
    steps, count_rows = rows_ref.shape[1], rows_ref.shape[2]
    width = head_ref.shape[2]

    def x_copy(i):
        part = pl.ds(pl.multiple_of(i * tile, tile), tile)
        return pltpu.make_async_copy(x_hbm.at[0, part], x_buf.at[part], x_sem.at[i])

    for i in range(tiles):
        x_copy(i).start()

    blocks = pool // LANES
    for step in range(steps):
        rows = rows_ref[0, step : step + 1, :]
        outer = lax.shift_right_logical(rows, 7)
        inner = lax.bitwise_and(rows, LANES - 1)
        one_outer = (lax.broadcasted_iota(jnp.int32, (blocks, count_rows), 0) == outer).astype(jnp.float32).astype(jnp.bfloat16)
        one_inner = (lax.broadcasted_iota(jnp.int32, (LANES, count_rows), 0) == inner).astype(jnp.float32).astype(jnp.bfloat16)
        table = lax.dot_general(one_inner, one_outer, (((1,), (1,)), ((), ())), preferred_element_type=jnp.float32)
        for j in range(blocks):
            drawn[step, j * LANES : (j + 1) * LANES, :] = jnp.broadcast_to(table[:, j : j + 1], (LANES, LANES))

    high, low = halves(head_ref[0])
    w_hi[...] = high
    w_lo[...] = low
    delta_ref[...] = jnp.zeros_like(delta_ref)
    scale = -LR / count_rows

    for step in range(steps):

        @pl.loop(0, tiles)
        def _(i):
            part = pl.ds(pl.multiple_of(i * tile, tile), tile)
            if step == 0:
                x_copy(i).wait()
                hidden = jnp.tanh(dot(x_buf[part, :], lower_ref[0]))
                h_hi, h_lo = halves(hidden)
                hid_hi[part, :] = h_hi
                hid_lo[part, :] = h_lo
            else:
                h_hi = hid_hi[part, :]
                h_lo = hid_lo[part, :]
            err = dot(h_hi, w_hi[...]) + dot(h_hi, w_lo[...]) + dot(h_lo, w_hi[...])
            err = err - target_ref[0, part, :].astype(jnp.float32)
            times = drawn[step, part, :]
            err = err * jnp.concatenate([times] * (width // LANES), axis=1) * scale
            e_hi, e_lo = halves(err)
            delta_ref[...] += dot_rows(h_hi, e_hi) + dot_rows(h_hi, e_lo) + dot_rows(h_lo, e_hi)

        if step + 1 < steps:
            high, low = halves(head_ref[0] + delta_ref[...])
            w_hi[...] = high
            w_lo[...] = low


def local_delta(features, targets, lower_weight, head_weight, batch_rows):
    pool, features_in = features.shape[1:]
    hid, out = head_weight.shape[1:]
    vmem = pl.BlockSpec(memory_space=pltpu.VMEM)
    tiles = pool // min(TILE, pool)
    return pl.pallas_call(
        local_kernel,
        name="local_steps",
        out_shape=jax.ShapeDtypeStruct((hid, out), jnp.float32),
        in_specs=[pl.BlockSpec(memory_space=pl.ANY), vmem, vmem, vmem, vmem],
        out_specs=vmem,
        scratch_shapes=[
            pltpu.VMEM((pool, features_in), jnp.bfloat16),
            pltpu.VMEM((pool, hid), jnp.bfloat16),
            pltpu.VMEM((pool, hid), jnp.bfloat16),
            pltpu.VMEM((batch_rows.shape[1], pool, LANES), jnp.float32),
            pltpu.VMEM((hid, out), jnp.bfloat16),
            pltpu.VMEM((hid, out), jnp.bfloat16),
            pltpu.SemaphoreType.DMA((tiles,)),
        ],
        compiler_params=pltpu.CompilerParams(vmem_limit_bytes=40 * 2**20),
    )(features, lower_weight, targets, head_weight, batch_rows)


def mean_kernel(
    sizes, chunks, id_ref, count_ref, delta_ref, out_ref,
    facts, chosen, inbox, own, from_left, from_right, to_right, to_left, outbox, result,
    fact_send, fact_recv, share_send, share_recv, right_send, right_recv, left_send, left_recv, back_send, back_recv,
):
    chip_count, board_count, cuts_count = sizes
    plane = chip_count * cuts_count
    number = plane * board_count
    chip, board, cuts = lax.axis_index("chip"), lax.axis_index("board"), lax.axis_index("cuts")
    seat = chip * cuts_count + cuts
    me = board * plane + seat
    hid, width = delta_ref.shape
    block = hid // chunks
    share = block // plane

    def at(board_index, seat_index):
        return (seat_index // cuts_count, board_index, lax.rem(seat_index, cuts_count))

    def rows_of(k, seat_index):
        return pl.ds(pl.multiple_of(k * block + seat_index * share, 8), share)

    barrier = pltpu.get_barrier_semaphore()

    def greet(offset, carry):
        other = lax.rem(me + offset, number)
        pl.semaphore_signal(barrier, inc=1, device_id=at(other // plane, lax.rem(other, plane)), device_id_type=MESH)
        return carry

    lax.fori_loop(1, number, greet, 0)
    kind = lax.broadcasted_iota(jnp.int32, (CLUSTERS, LANES), 0)
    facts[me] = jnp.where(kind == id_ref[0], count_ref[0].astype(jnp.float32), 0.0)
    pl.semaphore_wait(barrier, number - 1)

    def tell(offset, carry):
        other = lax.rem(me + offset, number)
        pltpu.make_async_remote_copy(
            src_ref=facts.at[me], dst_ref=facts.at[me], send_sem=fact_send, recv_sem=fact_recv,
            device_id=at(other // plane, lax.rem(other, plane)), device_id_type=MESH,
        ).start()
        return carry

    lax.fori_loop(1, number, tell, 0)

    for k in range(chunks):

        def give(offset, carry, k=k):
            other = lax.rem(seat + offset, plane)
            pltpu.make_async_remote_copy(
                src_ref=delta_ref.at[rows_of(k, other)], dst_ref=inbox.at[k, seat],
                send_sem=share_send, recv_sem=share_recv.at[k],
                device_id=at(board, other), device_id_type=MESH,
            ).start()
            return carry

        lax.fori_loop(1, plane, give, 0)
        inbox[k, seat] = delta_ref[rows_of(k, seat), :]

    def arrived(ref, sem):
        pltpu.make_async_copy(ref, ref, sem).wait()

    arrived(facts.at[pl.ds(0, number - 1)], fact_recv)
    counts = jnp.sum(facts[...], axis=0)
    inverse = 1.0 / (LR * jnp.maximum(counts, 1.0))
    for t in range(plane):
        chosen[t] = jnp.where(facts[board * plane + t] > 0, inverse, 0.0)

    def wide(row):
        return jnp.concatenate([row] * (width // LANES), axis=1)

    def right_copy(k):
        return pltpu.make_async_remote_copy(
            src_ref=to_right.at[k], dst_ref=from_left.at[k], send_sem=right_send.at[k], recv_sem=right_recv.at[k],
            device_id=at(board + 1, seat), device_id_type=MESH,
        )

    def left_copy(k):
        return pltpu.make_async_remote_copy(
            src_ref=to_left.at[k], dst_ref=from_right.at[k], send_sem=left_send.at[k], recv_sem=left_recv.at[k],
            device_id=at(board - 1, seat), device_id_type=MESH,
        )

    last = board_count - 1

    def add_up(k):
        arrived(inbox.at[k, pl.ds(0, plane - 1)], share_recv.at[k])
        sums = [jnp.zeros((share, width), jnp.float32)] * CLUSTERS
        for t in range(plane):
            value = inbox[k, t]
            for c in range(CLUSTERS):
                sums[c] = sums[c] + wide(facts[board * plane + t, c : c + 1, :]) * value
        for c in range(CLUSTERS):
            own[k, c] = sums[c]

    def pass_right(k):
        @pl.when(board == 0)
        def _():
            from_left[k] = jnp.zeros_like(from_left[k])

        @pl.when(board > 0)
        def _():
            arrived(from_left.at[k], right_recv.at[k])

        @pl.when(board < last)
        def _():
            to_right[k] = own[k] + from_left[k]
            right_copy(k).start()

    def pass_left(k):
        @pl.when(board == last)
        def _():
            from_right[k] = jnp.zeros_like(from_right[k])

        @pl.when(board < last)
        def _():
            arrived(from_right.at[k], left_recv.at[k])

        @pl.when(board > 0)
        def _():
            to_left[k] = own[k] + from_right[k]
            left_copy(k).start()

    def give_back(k):
        total = [own[k, c] + from_left[k, c] + from_right[k, c] for c in range(CLUSTERS)]
        for t in range(plane):
            value = wide(chosen[t, 0:1, :]) * total[0]
            for c in range(1, CLUSTERS):
                value = value + wide(chosen[t, c : c + 1, :]) * total[c]
            outbox[k, t] = value
        result[rows_of(k, seat), :] = outbox[k, seat]

        def give(offset, carry):
            other = lax.rem(seat + offset, plane)
            pltpu.make_async_remote_copy(
                src_ref=outbox.at[k, other], dst_ref=result.at[rows_of(k, seat)],
                send_sem=back_send, recv_sem=back_recv,
                device_id=at(board, other), device_id_type=MESH,
            ).start()
            return carry

        lax.fori_loop(1, plane, give, 0)

    right_lag = LAG * board
    left_lag = LAG * (last - board)
    back_lag = jnp.maximum(right_lag, left_lag)

    def tick(step, carry):
        for lag, act in ((0, add_up), (right_lag, pass_right), (left_lag, pass_left), (back_lag, give_back)):
            k = step - lag

            @pl.when((k >= 0) & (k < chunks))
            def _():
                act(k)

        return carry

    lax.fori_loop(0, chunks + LAG * last, tick, 0)

    moved = pl.ds(0, chunks * (plane - 1) * share)
    arrived(result.at[moved], back_recv)
    out_ref[0] = result[...]
    arrived(result.at[moved], back_send)
    arrived(result.at[moved], share_send)
    arrived(facts.at[pl.ds(0, number - 1)], fact_send)

    @pl.when(board < last)
    def _():
        for k in range(chunks):
            arrived(to_right.at[k], right_send.at[k])

    @pl.when(board > 0)
    def _():
        for k in range(chunks):
            arrived(to_left.at[k], left_send.at[k])


def cluster_mean(sizes, delta, sample_counts, cluster_ids):
    hid, width = delta.shape
    plane = sizes[0] * sizes[2]
    number = plane * sizes[1]
    chunks = max(1, min(CHUNKS, hid // (plane * 8)))
    share = hid // (chunks * plane)
    vmem = pl.BlockSpec(memory_space=pltpu.VMEM)
    smem = pl.BlockSpec(memory_space=pltpu.SMEM)
    sums = pltpu.VMEM((chunks, CLUSTERS, share, width), jnp.float32)
    shares = pltpu.VMEM((chunks, plane, share, width), jnp.float32)
    one, many = pltpu.SemaphoreType.DMA, pltpu.SemaphoreType.DMA((chunks,))
    return pl.pallas_call(
        functools.partial(mean_kernel, sizes, chunks),
        name="cluster_mean",
        out_shape=jax.ShapeDtypeStruct((1, hid, width), jnp.float32),
        in_specs=[smem, smem, vmem],
        out_specs=vmem,
        scratch_shapes=[
            pltpu.VMEM((number, CLUSTERS, LANES), jnp.float32),
            pltpu.VMEM((plane, CLUSTERS, LANES), jnp.float32),
            shares, sums, sums, sums, sums, sums, shares,
            pltpu.VMEM((hid, width), jnp.float32),
            one, one, one, many, many, many, many, many, one, one,
        ],
        compiler_params=pltpu.CompilerParams(collective_id=0, has_side_effects=True, vmem_limit_bytes=40 * 2**20),
    )(cluster_ids, sample_counts, delta)


def solution(mesh):
    sizes = (mesh.shape["chip"], mesh.shape["board"], mesh.shape["cuts"])

    def on_device(features, targets, lower_weight, head_weight, batch_rows, sample_counts, cluster_ids):
        delta = local_delta(features, targets, lower_weight, head_weight, batch_rows)
        return cluster_mean(sizes, delta, sample_counts, cluster_ids)

    rows, flat = P(("chip", "board", "cuts"), None, None), P(("chip", "board", "cuts"))
    return jax.shard_map(
        on_device,
        mesh=mesh,
        in_specs=(rows, rows, rows, rows, rows, flat, flat),
        out_specs=rows,
        check_vma=False,
    )
```

time: 139 us -> 68.7 us (0.49)
  blocking collectives: 62.6 us -> 0 us
  Pallas kernels: 0 us -> 59.9 us
  local copies, waits for them, and re-layouts: 29.7 us -> 7.16 us
  matrix products: 20.5 us -> 0 us
  waiting for transfers between devices: 13 us -> 0 us
  starting transfers between devices: 10.4 us -> 0 us
    pallas_call x0 -> x2, Pallas kernels: none -> 59.9 us  [the longest x1 38.2 us: cluster_mean(): pl.pallas_call(functools.partial(mean_kernel, sizes, chunks), name='clust...]
    unnamed x1 -> x0, blocking collectives: 40 us -> none
    gather x4 -> x0, local copies, waits for them, and re-layouts: 23.9 us -> none  [the longest x2 15 us: on_device(): picked = jnp.take(hidden, batch_rows[0, step], axis=0)]
    all_to_all x2 -> x0, blocking collectives: 22.6 us -> none  [the longest x1 12.1 us: on_device(): lax.all_to_all(scaled, 'chip', split_axis=0, concat_axis=0, tiled=True)]
    dot_general x7 -> x0, matrix products: 20.5 us -> none  [the longest x2 7.26 us: on_device(): grad = jnp.dot(picked.T, err, precision=lax.Precision.HIGHEST) / count_rows]
    all_to_all x2 -> x0, waiting for transfers between devices: 13 us -> none  [the longest x1 13 us: on_device(): lax.all_to_all(lax.all_to_all(outgoing, 'chip', split_axis=0, concat_axis...]
    all_to_all x2 -> x0, starting transfers between devices: 10.4 us -> none  [the longest x1 5.94 us: on_device(): lax.all_to_all(lax.all_to_all(scaled, 'chip', split_axis=0, concat_axis=0...]
    unnamed x14 -> x11, local copies, waits for them, and re-layouts: 0.65 us -> 7.16 us
  transfers between devices with their start and end apart: 2 -> 0, of which waited for: 1 -> 0; matrix products, arithmetic and copies ran while one was open for 1% -> 0% of each run, Pallas kernels for 0% -> 0%
where the time goes in v1:
time: 68.7 us; the launch traced here: 68.3 us
  Pallas kernels  59.9 us (87%)
  local copies, waits for them, and re-layouts  7.16 us (10%)
  between operations  1.33 us (2%)
    pallas_call x1, Pallas kernels, cluster_mean(): pl.pallas_call(functools.partial(mean_kernel, sizes, chunks), name='clust...  38.2 us
    pallas_call x1, Pallas kernels, local_delta(): pl.pallas_call(local_kernel, name='local_steps', out_shape=jax.ShapeDtype...  21.6 us
    unnamed x11, local copies, waits for them, and re-layouts  7.16 us

profile of v1, /device:TPU:0, one launch (start us, length us, event | category | flops | bytes accessed | tf_op | source)
XLA Modules:
  0.0 68.3 jit_solution(7844255217363818168)
XLA Ops:
  1.3 0.0 copy-start
  1.3 2.2 %copy-done = bf16[1,2048,1024]{2,1,0:T(8,128)(2,1)S(1)} copy-done((bf16[1,2048,1024]{2,1,0:T(8,128)(2,1)S(1)}, bf16[1,2048,1024]{2,1,0:T(8,128)(2,1)}, u32[]{:S(2)}) %copy-start) | copy-done | bytes 4194328
  3.5 0.0 copy-start.1
  3.5 1.2 %copy-done.1 = bf16[1,1024,512]{2,1,0:T(8,128)(2,1)S(1)} copy-done((bf16[1,1024,512]{2,1,0:T(8,128)(2,1)S(1)}, bf16[1,1024,512]{2,1,0:T(8,128)(2,1)}, u32[]{:S(2)}) %copy-start.1) | copy-done | bytes 1048600
  4.7 0.0 copy-start.2
  4.7 1.2 %copy-done.2 = bf16[1,2048,256]{2,1,0:T(8,128)(2,1)S(1)} copy-done((bf16[1,2048,256]{2,1,0:T(8,128)(2,1)S(1)}, bf16[1,2048,256]{2,1,0:T(8,128)(2,1)}, u32[]{:S(2)}) %copy-start.2) | copy-done | bytes 1048600
  5.9 0.0 copy-start.3
  5.9 1.0 %copy-done.3 = f32[1,512,256]{2,1,0:T(8,128)S(1)} copy-done((f32[1,512,256]{2,1,0:T(8,128)S(1)}, f32[1,512,256]{2,1,0:T(8,128)}, u32[]{:S(2)}) %copy-start.3) | copy-done | bytes 524312
  7.0 0.0 copy-start.4
  7.0 0.7 %copy-done.4 = s32[1,2,1024]{2,1,0:T(2,128)S(1)} copy-done((s32[1,2,1024]{2,1,0:T(2,128)S(1)}, s32[1,2,1024]{2,1,0:T(2,128)}, u32[]{:S(2)}) %copy-start.4) | copy-done | bytes 8216
  7.7 21.6 %local_steps.1.delta_ref = f32[512,256]{1,0:T(8,128)S(1)} custom-call(bf16[1,2048,1024]{2,1,0:T(8,128)(2,1)S(1)} %copy-done, bf16[1,1024,512]{2,1,0:T(8,128)(2,1)S(1)} %copy-done.1, bf16[1,2048,256]{2,1,0:T(8,128)(2,1)S(1)} %copy-done.2, f32[1,512,256]{2,1,0:T(8,128)S(1)} %copy-done.3, s32[1,2,1024]{2,1,0:T(2,128)S(1)} %copy-done.4), custom_call_target="tpu_custom_call" | custom-call | tf_op jit(solution)/shard_map/local_steps/pallas_call | solution.py:96
  29.3 38.2 %cluster_mean.1 = f32[1,512,256]{2,1,0:T(8,128)S(1)} custom-call(s32[1]{0:T(128)S(6)} %copy.10.id_ref, s32[1]{0:T(128)S(6)} %copy.9.count_ref, f32[512,256]{1,0:T(8,128)S(1)} %local_steps.1.delta_ref), custom_call_target="tpu_custom_call" | custom-call | tf_op jit(solution)/shard_map/cluster_mean/pallas_call | solution.py:301
  67.6 0.8 %copy.11 = f32[1,512,256]{2,1,0:T(8,128)} copy(f32[1,512,256]{2,1,0:T(8,128)S(1)} %cluster_mean.1) | data formatting | bytes 1048576
Async XLA Ops:
  1.3 2.2 %copy-start = (bf16[1,2048,1024]{2,1,0:T(8,128)(2,1)S(1)}, bf16[1,2048,1024]{2,1,0:T(8,128)(2,1)}, u32[]{:S(2)}) copy-start(bf16[1,2048,1024]{2,1,0:T(8,128)(2,1)} %x_hbm.1) | copy-start | bytes 12582916
  3.5 1.2 %copy-start.1 = (bf16[1,1024,512]{2,1,0:T(8,128)(2,1)S(1)}, bf16[1,1024,512]{2,1,0:T(8,128)(2,1)}, u32[]{:S(2)}) copy-start(bf16[1,1024,512]{2,1,0:T(8,128)(2,1)} %lower_ref.1) | copy-start | bytes 3145732
  4.7 1.2 %copy-start.2 = (bf16[1,2048,256]{2,1,0:T(8,128)(2,1)S(1)}, bf16[1,2048,256]{2,1,0:T(8,128)(2,1)}, u32[]{:S(2)}) copy-start(bf16[1,2048,256]{2,1,0:T(8,128)(2,1)} %target_ref.1) | copy-start | bytes 3145732
  5.9 1.0 %copy-start.3 = (f32[1,512,256]{2,1,0:T(8,128)S(1)}, f32[1,512,256]{2,1,0:T(8,128)}, u32[]{:S(2)}) copy-start(f32[1,512,256]{2,1,0:T(8,128)} %head_ref.1) | copy-start | bytes 1572868
  7.0 0.7 %copy-start.4 = (s32[1,2,1024]{2,1,0:T(2,128)S(1)}, s32[1,2,1024]{2,1,0:T(2,128)}, u32[]{:S(2)}) copy-start(s32[1,2,1024]{2,1,0:T(2,128)} %rows_ref.1) | copy-start | bytes 24580
